TPU v7x, 512 devices: a whole 4x4x16 slice. The times are simulated.
512 devices in a mesh: utt: 8 (over y, z_hi), tm: 64 (over x, z_lo, core).
Axes of the slice: x: 4, y: 4, z: 16 (z_hi: 2, z_lo: 8; z = z_hi * 8 + z_lo), core: 2. Of those that a mesh axis runs over, the one named last changes fastest.
Arguments:
- stem: bfloat16 [65536, 1280], P(('utt', 'tm')), parts along dimension 0, may hold values from -8 to 8
- norm_gain: float32 [1280], replicated, may hold values from 0.25 to 1.75
- qkv_weight: bfloat16 [1280, 3840], P('tm'), may hold values from -0.2934839 to 0.2934839
- segment_ids: int32 [65536], P(('utt', 'tm')), parts along dimension 0, may hold values from 1 to 21, as said below
- dec_queries: bfloat16 [1024, 1280], P(('utt', 'tm')), parts along dimension 0, may hold values from -9 to 9
- stretch_mask: int32 [1024, 64], P(('utt', 'tm')), parts along dimension 0, may hold values 0 or 1
Outputs:
- memory: bfloat16 [65536, 1280], P(('utt', 'tm')), parts along dimension 0
- cross_out: bfloat16 [1024, 1280], P(('utt', 'tm')), parts along dimension 0
There are 8 independent parts, one for each index of `utt`. A program takes and returns all parts, laid end to end along the dimension named above; an argument that names none is the same for every part. Nothing has to cross between parts.
Inputs may be any that keep to these rules, and one draw needn't show every extreme that they name: `segment_ids`: ids start at 1 and rise by one from run to run; each id covers one contiguous run of at most 512 positions, and the last run is exactly 512 positions long.
All inputs are finite; a program needn't handle non-finite values. No bound on the sum of `stretch_mask` on one device may be relied on, other than what follows from the above.
Results may differ from a plain program's by a relative error of at most 0.0062.
Values may be sent and summed in bfloat16 or wider, within the bound.
A program may use at most 64 MiB of HBM per device.

v0:
```python
import math
import jax
import jax.numpy as jnp
from jax import lax
from jax.sharding import PartitionSpec as P

HD = 64


def from_behind(block, axis, distance):
    devices = range(lax.axis_size(axis))
    route = [(i - distance, i) for i in devices if i - distance in devices]
    return lax.ppermute(block, axis, route)


def on_device(stem, norm_gain, qkv_weight, segment_ids, dec_queries, stretch_mask):
    rows, width = stem.shape
    heads = width // HD
    scale = HD ** (-0.5)
    values_in = stem.astype(jnp.float32)
    mean = jnp.mean(values_in, axis=-1, keepdims=True)
    var = jnp.mean((values_in - mean) ** 2, axis=-1, keepdims=True)
    normed = ((values_in - mean) * lax.rsqrt(var + 1e-05) * norm_gain).astype(jnp.bfloat16)
    projected = jnp.dot(
        normed,
        lax.all_gather(qkv_weight, "tm", axis=0, tiled=True),
        preferred_element_type=jnp.float32,
    ).astype(jnp.bfloat16)
    query_part = projected[:, :width]
    keyvals = projected[:, width:]
    kv_pieces = []
    seg_pieces = []
    for offset in range(-4, 5):
        if offset == 0:
            kv_pieces.append(keyvals)
            seg_pieces.append(segment_ids)
        else:
            kv_pieces.append(from_behind(keyvals, "tm", -offset))
            seg_pieces.append(from_behind(segment_ids, "tm", -offset))
    extended = jnp.concatenate(kv_pieces, axis=0)
    seg_wide = jnp.concatenate(seg_pieces, axis=0)
    same = segment_ids[:, None] == seg_wide[None, :]
    group = math.gcd(heads, 4)
    span = group * HD
    groups = heads // group

    def attend(index):
        start = index * span
        query_group = lax.dynamic_slice_in_dim(query_part, start, span, 1).reshape(rows, group, HD)
        key_group = lax.dynamic_slice_in_dim(extended, start, span, 1).reshape(-1, group, HD)
        value_group = lax.dynamic_slice_in_dim(extended, width + start, span, 1).reshape(
            -1, group, HD
        )
        scores = (
            jnp.einsum("qhd,khd->hqk", query_group, key_group, preferred_element_type=jnp.float32)
            * scale
        )
        scores = jnp.where(same[None], scores, jnp.float32(-1e30))
        top = jnp.max(scores, axis=-1, keepdims=True)
        raised = jnp.exp(scores - top)
        probs = (raised / jnp.sum(raised, axis=-1, keepdims=True)).astype(jnp.bfloat16)
        context = jnp.einsum("hqk,khd->qhd", probs, value_group, preferred_element_type=jnp.float32)
        return context.reshape(rows, span)

    contexts = lax.map(attend, jnp.arange(groups, dtype=jnp.int32))
    context = jnp.transpose(contexts, (1, 0, 2)).reshape(rows, width)
    memory = (values_in + context).astype(jnp.bfloat16)
    tokens_dev = dec_queries.shape[0]
    all_queries = lax.all_gather(dec_queries, "tm", axis=0, tiled=True)
    all_masks = lax.all_gather(stretch_mask, "tm", axis=0, tiled=True)
    total_tokens = all_queries.shape[0]
    device = lax.axis_index("tm")
    column = lax.dynamic_slice_in_dim(all_masks, device, 1, 1)[:, 0]
    owner = jnp.arange(total_tokens, dtype=jnp.int32) // tokens_dev
    allowed = (column == 1) | (owner == device)
    query_heads = all_queries.reshape(total_tokens, heads, HD)
    memory_heads = memory.reshape(rows, heads, HD)
    cross = (
        jnp.einsum("thd,phd->htp", query_heads, memory_heads, preferred_element_type=jnp.float32)
        * scale
    )
    local_top = jnp.max(cross, axis=-1)
    weights = jnp.where(
        allowed[None, :, None], jnp.exp(cross - local_top[:, :, None]), jnp.float32(0.0)
    )
    denom = jnp.transpose(jnp.sum(weights, axis=-1))
    numer = jnp.einsum(
        "htp,phd->thd",
        weights.astype(jnp.bfloat16),
        memory_heads,
        preferred_element_type=jnp.float32,
    )
    top_masked = jnp.transpose(jnp.where(allowed[None, :], local_top, jnp.float32(-1e30)))
    num_all, top_all, den_all = (
        lax.all_to_all(numer[None], "tm", split_axis=1, concat_axis=0, tiled=True),
        lax.all_to_all(top_masked[None], "tm", split_axis=1, concat_axis=0, tiled=True),
        lax.all_to_all(denom[None], "tm", split_axis=1, concat_axis=0, tiled=True),
    )
    best = jnp.max(top_all, axis=0)
    factor = jnp.exp(top_all - best[None])
    num_total = jnp.sum(factor[..., None] * num_all, axis=0)
    den_total = jnp.sum(factor * den_all, axis=0)
    cross_out = (num_total / den_total[..., None]).reshape(tokens_dev, width).astype(jnp.bfloat16)
    return (memory, cross_out)


def solution(mesh):
    placed = (
        P(("utt", "tm"), None),
        P(),
        P("tm", None),
        P(("utt", "tm")),
        P(("utt", "tm"), None),
        P(("utt", "tm"), None),
    )
    return jax.shard_map(
        on_device,
        mesh=mesh,
        in_specs=placed,
        out_specs=(P(("utt", "tm"), None), P(("utt", "tm"), None)),
        check_vma=False,
    )
```

profile of v0, /device:TPU:1, one launch (start us, length us, event | category | flops | bytes accessed | tf_op | source)
XLA Modules:
  0.0 600.4 jit_solution(3820719611877599102)
XLA Ops:
  10.5 8.7 %collective-permute-start.12 = (s32[128]{0:T(128)}, s32[128]{0:T(128)S(1)}, u32[]{:S(2)}, u32[]{:S(2)}) collective-permute-start(s32[128]{0:T(128)} %param.11), channel_id=1, source_target_pairs={{1,0},{2,1},{3,2},{4,3},{5,4},{6,5},{7,6},{8,7},{9,8},{10,9},{11,1... | collective-permute-start | bytes 1544 | tf_op jit(solution)/shard_map/ppermute | solution.py:13
  19.3 4.2 collective-permute-start.11
  23.4 5.2 collective-permute-start.8
  28.6 116.4 %all-gather.1 = s32[64,2,64]{2,1,0:T(2,128)S(1)} all-gather(s32[1,2,64]{2,1,0:T(2,128)} %bitcast.74), channel_id=1, replica_groups=mesh['utt'=8,'tm'=64] {'tm'}, dimensions={0}, use_global_device_ids=true | all-gather | bytes 33280 | tf_op jit(solution)/shard_map/all_gather | solution.py:70
  146.7 114.0 %all-gather.2 = bf16[64,2,1280]{2,1,0:T(2,128)(2,1)S(1)} all-gather(bf16[1,2,1280]{2,1,0:T(2,128)(2,1)} %bitcast.73), channel_id=1, replica_groups=mesh['utt'=8,'tm'=64] {'tm'}, dimensions={0}, use_global_device_ids=true | all-gather | bytes 332800 | tf_op jit(solution)/shard_map/all_gather | solution.py:69
  263.4 6.1 %collective-permute-start.10 = (s32[128]{0:T(128)S(1)}, s32[128]{0:T(128)S(1)}, u32[]{:S(2)}, u32[]{:S(2)}) collective-permute-start(s32[128]{0:T(128)S(1)} %copy-done.1), channel_id=1, source_target_pairs={{0,2},{1,3},{2,4},{3,5},{4,6},{5,7},{6,8},{7,9},{8,10},{9,11},{10,... | collective-permute-start | bytes 1544 | tf_op jit(solution)/shard_map/ppermute | solution.py:13
  271.5 13.7 %reshape.128 = bf16[1280,3840]{1,0:T(8,128)(2,1)} reshape(bf16[64,20,3840]{2,1,0:T(8,128)(2,1)} %all-gather.5.cloned.1.call-done) | data formatting | bytes 19660800
  285.2 5.3 convolution_convert_fusion
  290.6 4.9 collective-permute-start
  295.6 5.5 collective-permute-start.1
  305.1 4.9 collective-permute-done
  310.0 24.2 %collective-permute-start.2 = (bf16[128,2560]{1,0:T(8,128)(2,1)S(1)}, bf16[128,2560]{1,0:T(8,128)(2,1)S(1)}, u32[]{:S(2)}, u32[]{:S(2)}) collective-permute-start(bf16[128,2560]{1,0:T(8,128)(2,1)S(1)} %slice.8), channel_id=1, source_target_pairs={{0,2},{1,3},{2,4},{3,5},{4,6},{5,7},{6,8},{7,9},{8,10},{9,11},{10,... | collective-permute-start | bytes 1966088 | tf_op jit(solution)/shard_map/ppermute | solution.py:13
  335.1 13.4 %collective-permute-start.3 = (bf16[128,2560]{1,0:T(8,128)(2,1)S(1)}, bf16[128,2560]{1,0:T(8,128)(2,1)S(1)}, u32[]{:S(2)}, u32[]{:S(2)}) collective-permute-start(bf16[128,2560]{1,0:T(8,128)(2,1)S(1)} %slice.8), channel_id=1, source_target_pairs={{0,1},{1,2},{2,3},{3,4},{4,5},{5,6},{6,7},{7,8},{8,9},{9,10},{10,1... | collective-permute-start | bytes 1966088 | tf_op jit(solution)/shard_map/ppermute | solution.py:13
  352.2 3.8 collective-permute-done.3
  357.9 53.3 %collective-permute-done.4 = bf16[128,2560]{1,0:T(8,128)(2,1)S(1)} collective-permute-done((bf16[128,2560]{1,0:T(8,128)(2,1)S(1)}, bf16[128,2560]{1,0:T(8,128)(2,1)S(1)}, u32[]{:S(2)}, u32[]{:S(2)}) %collective-permute-start.4) | collective-permute-done | bytes 655392 | tf_op jit(solution)/shard_map/ppermute | solution.py:13
  413.0 11.1 %collective-permute-done.6 = bf16[128,2560]{1,0:T(8,128)(2,1)S(1)} collective-permute-done((bf16[128,2560]{1,0:T(8,128)(2,1)S(1)}, bf16[128,2560]{1,0:T(8,128)(2,1)S(1)}, u32[]{:S(2)}, u32[]{:S(2)}) %collective-permute-start.6) | collective-permute-done | bytes 655392 | tf_op jit(solution)/shard_map/ppermute | solution.py:13
  425.9 8.9 %copy.40 = bf16[1152,2560]{0,1:T(8,128)(2,1)} copy(bf16[1152,2560]{1,0:T(8,128)(2,1)} %constant_dynamic-update-slice_fusion.1) | data formatting | bytes 11796480
  434.8 41.2 %while.13 = (s32[]{:T(128)}, f32[5,128,256]{1,2,0:T(8,128)}, s32[5]{0:T(128)S(1)}, bf16[1152,2560]{0,1:T(8,128)(2,1)}, bf16[128,1280]{1,0:T(8,128)(2,1)S(1)}, /*...) while((s32[]{:T(128)}, f32[5,128,256]{1,2,0:T(8,128)}, ...), condition=%wide.region_5.6_spmd.clone, body=%wide.region_2.5_spmd.clone.sunk | while | flops 154682496 | bytes 9282826 | solution.py:65
  478.7 32.9 %all-to-all-start.2 = ((f32[1,128,20]{2,0,1:T(1,128)}), f32[1,128,20]{2,0,1:T(1,128)S(1)}, u32[]{:S(2)}, u32[]{:S(2)}) async-start(f32[1,128,20]{2,0,1:T(1,128)} %copy.49), calls=%async_computation.2 | async-start | bytes 131072 | tf_op jit(solution)/shard_map/all_to_all | solution.py:97
  512.4 12.1 %all-to-all-done.2 = f32[1,128,20]{2,0,1:T(1,128)S(1)} async-done(((f32[1,128,20]{2,0,1:T(1,128)}), f32[1,128,20]{2,0,1:T(1,128)S(1)}, u32[]{:S(2)}, u32[]{:S(2)}) %all-to-all-start.2) | async-done | bytes 10272 | tf_op jit(solution)/shard_map/all_to_all | solution.py:97
  524.5 5.0 all-to-all-start
  533.7 3.9 reduce
  542.3 10.1 %all-to-all-start.1 = ((f32[64,1,2560]{2,1,0:T(1,128)}), f32[64,1,2560]{2,1,0:T(1,128)S(1)}, u32[]{:S(2)}, u32[]{:S(2)}) async-start(f32[64,1,2560]{2,1,0:T(1,128)} %reshape.137), calls=%async_computation.1 | async-start | bytes 1310720 | tf_op jit(solution)/shard_map/all_to_all | solution.py:95
  554.3 32.7 %all-to-all-done.1 = f32[64,1,2560]{2,1,0:T(1,128)S(1)} async-done(((f32[64,1,2560]{2,1,0:T(1,128)}), f32[64,1,2560]{2,1,0:T(1,128)S(1)}, u32[]{:S(2)}, u32[]{:S(2)}) %all-to-all-start.1) | async-done | bytes 655392 | tf_op jit(solution)/shard_map/all_to_all | solution.py:95
  (125 shorter events, 82.0 us)
Async XLA Ops:
  7.2 254.2 %copy-start.1 = (s32[128]{0:T(128)S(1)}, s32[128]{0:T(128)}, u32[]{:S(2)}) copy-start(s32[128]{0:T(128)} %param.11) | copy-start | bytes 1540
  7.2 264.3 %all-gather.5.cloned.1.call-start = ((), (), s32[]{:S(2)}) async-start(), calls=%async_computation.3 | async-start | bytes 11980800 | tf_op jit(solution)/shard_map/all_gather | solution.py:26
  7.9 293.2 %collective-permute-start.14 = (s32[128]{0:T(128)}, s32[128]{0:T(128)S(1)}, u32[]{:S(2)}, u32[]{:S(2)}) collective-permute-start(s32[128]{0:T(128)} %param.11), channel_id=1, source_target_pairs={{3,0},{4,1},{5,2},{6,3},{7,4},{8,5},{9,6},{10,7},{11,8},{12,9},{13... | collective-permute-start | bytes 1544 | tf_op jit(solution)/shard_map/ppermute | solution.py:13
  9.2 291.9 %collective-permute-start.13 = (s32[128]{0:T(128)}, s32[128]{0:T(128)S(1)}, u32[]{:S(2)}, u32[]{:S(2)}) collective-permute-start(s32[128]{0:T(128)} %param.11), channel_id=1, source_target_pairs={{2,0},{3,1},{4,2},{5,3},{6,4},{7,5},{8,6},{9,7},{10,8},{11,9},{12,... | collective-permute-start | bytes 1544 | tf_op jit(solution)/shard_map/ppermute | solution.py:13
  10.5 285.0 %collective-permute-start.12 = (s32[128]{0:T(128)}, s32[128]{0:T(128)S(1)}, u32[]{:S(2)}, u32[]{:S(2)}) collective-permute-start(s32[128]{0:T(128)} %param.11), channel_id=1, source_target_pairs={{1,0},{2,1},{3,2},{4,3},{5,4},{6,5},{7,6},{8,7},{9,8},{10,9},{11,1... | collective-permute-start | bytes 1544 | tf_op jit(solution)/shard_map/ppermute | solution.py:13
  19.3 271.3 %collective-permute-start.11 = (s32[128]{0:T(128)}, s32[128]{0:T(128)S(1)}, u32[]{:S(2)}, u32[]{:S(2)}) collective-permute-start(s32[128]{0:T(128)} %param.11), channel_id=1, source_target_pairs={{0,1},{1,2},{2,3},{3,4},{4,5},{5,6},{6,7},{7,8},{8,9},{9,10},{10,1... | collective-permute-start | bytes 1544 | tf_op jit(solution)/shard_map/ppermute | solution.py:13
  23.4 237.9 %collective-permute-start.8 = (s32[128]{0:T(128)}, s32[128]{0:T(128)S(1)}, u32[]{:S(2)}, u32[]{:S(2)}) collective-permute-start(s32[128]{0:T(128)} %param.11), channel_id=1, source_target_pairs={{0,4},{1,5},{2,6},{3,7},{4,8},{5,9},{6,10},{7,11},{8,12},{9,13},{1... | collective-permute-start | bytes 1544 | tf_op jit(solution)/shard_map/ppermute | solution.py:13
  261.4 2.0 collective-permute-start.9
  263.4 6.8 %collective-permute-start.10 = (s32[128]{0:T(128)S(1)}, s32[128]{0:T(128)S(1)}, u32[]{:S(2)}, u32[]{:S(2)}) collective-permute-start(s32[128]{0:T(128)S(1)} %copy-done.1), channel_id=1, source_target_pairs={{0,2},{1,3},{2,4},{3,5},{4,6},{5,7},{6,8},{7,9},{8,10},{9,11},{10,... | collective-permute-start | bytes 1544 | tf_op jit(solution)/shard_map/ppermute | solution.py:13
  270.2 31.0 %collective-permute-start.15 = (s32[128]{0:T(128)S(1)}, s32[128]{0:T(128)S(1)}, u32[]{:S(2)}, u32[]{:S(2)}) collective-permute-start(s32[128]{0:T(128)S(1)} %copy-done.1), channel_id=1, source_target_pairs={{4,0},{5,1},{6,2},{7,3},{8,4},{9,5},{10,6},{11,7},{12,8},{13,9},{1... | collective-permute-start | bytes 1544 | tf_op jit(solution)/shard_map/ppermute | solution.py:13
  271.5 13.7 %copy-start.2 = (f32[1280]{0:T(1024)S(1)}, f32[1280]{0:T(1024)}, u32[]{:S(2)}) copy-start(f32[1280]{0:T(1024)} %param.9) | copy-start | bytes 15364
  290.5 66.5 %copy-start = (bf16[128,3840]{1,0:T(8,128)(2,1)}, bf16[128,3840]{1,0:T(8,128)(2,1)S(1)}, u32[]{:S(2)}) copy-start(bf16[128,3840]{1,0:T(8,128)(2,1)S(1)} %convolution_convert_fusion) | copy-start | bytes 2949124
  290.6 19.4 %collective-permute-start = (bf16[128,2560]{1,0:T(8,128)(2,1)S(1)}, bf16[128,2560]{1,0:T(8,128)(2,1)S(1)}, u32[]{:S(2)}, u32[]{:S(2)}) collective-permute-start(bf16[128,2560]{1,0:T(8,128)(2,1)S(1)} %slice.8), channel_id=1, source_target_pairs={{0,4},{1,5},{2,6},{3,7},{4,8},{5,9},{6,10},{7,11},{8,12},{9,13},{1... | collective-permute-start | bytes 1966088 | tf_op jit(solution)/shard_map/ppermute | solution.py:13
  295.6 39.6 %collective-permute-start.1 = (bf16[128,2560]{1,0:T(8,128)(2,1)S(1)}, bf16[128,2560]{1,0:T(8,128)(2,1)S(1)}, u32[]{:S(2)}, u32[]{:S(2)}) collective-permute-start(bf16[128,2560]{1,0:T(8,128)(2,1)S(1)} %slice.8), channel_id=1, source_target_pairs={{0,3},{1,4},{2,5},{3,6},{4,7},{5,8},{6,9},{7,10},{8,11},{9,12},{10... | collective-permute-start | bytes 1966088 | tf_op jit(solution)/shard_map/ppermute | solution.py:13
  301.2 123.8 %collective-permute-start.7 = (bf16[128,2560]{1,0:T(8,128)(2,1)S(1)}, bf16[128,2560]{1,0:T(8,128)(2,1)S(1)}, u32[]{:S(2)}, u32[]{:S(2)}) collective-permute-start(bf16[128,2560]{1,0:T(8,128)(2,1)S(1)} %slice.8), channel_id=1, source_target_pairs={{4,0},{5,1},{6,2},{7,3},{8,4},{9,5},{10,6},{11,7},{12,8},{13,9},{1... | collective-permute-start | bytes 1966088 | tf_op jit(solution)/shard_map/ppermute | solution.py:13
  302.5 121.6 %collective-permute-start.6 = (bf16[128,2560]{1,0:T(8,128)(2,1)S(1)}, bf16[128,2560]{1,0:T(8,128)(2,1)S(1)}, u32[]{:S(2)}, u32[]{:S(2)}) collective-permute-start(bf16[128,2560]{1,0:T(8,128)(2,1)S(1)} %slice.8), channel_id=1, source_target_pairs={{3,0},{4,1},{5,2},{6,3},{7,4},{8,5},{9,6},{10,7},{11,8},{12,9},{13... | collective-permute-start | bytes 1966088 | tf_op jit(solution)/shard_map/ppermute | solution.py:13
  303.8 108.4 %collective-permute-start.5 = (bf16[128,2560]{1,0:T(8,128)(2,1)S(1)}, bf16[128,2560]{1,0:T(8,128)(2,1)S(1)}, u32[]{:S(2)}, u32[]{:S(2)}) collective-permute-start(bf16[128,2560]{1,0:T(8,128)(2,1)S(1)} %slice.8), channel_id=1, source_target_pairs={{2,0},{3,1},{4,2},{5,3},{6,4},{7,5},{8,6},{9,7},{10,8},{11,9},{12,... | collective-permute-start | bytes 1966088 | tf_op jit(solution)/shard_map/ppermute | solution.py:13
  310.0 39.5 %collective-permute-start.2 = (bf16[128,2560]{1,0:T(8,128)(2,1)S(1)}, bf16[128,2560]{1,0:T(8,128)(2,1)S(1)}, u32[]{:S(2)}, u32[]{:S(2)}) collective-permute-start(bf16[128,2560]{1,0:T(8,128)(2,1)S(1)} %slice.8), channel_id=1, source_target_pairs={{0,2},{1,3},{2,4},{3,5},{4,6},{5,7},{6,8},{7,9},{8,10},{9,11},{10,... | collective-permute-start | bytes 1966088 | tf_op jit(solution)/shard_map/ppermute | solution.py:13
  335.1 20.9 %collective-permute-start.3 = (bf16[128,2560]{1,0:T(8,128)(2,1)S(1)}, bf16[128,2560]{1,0:T(8,128)(2,1)S(1)}, u32[]{:S(2)}, u32[]{:S(2)}) collective-permute-start(bf16[128,2560]{1,0:T(8,128)(2,1)S(1)} %slice.8), channel_id=1, source_target_pairs={{0,1},{1,2},{2,3},{3,4},{4,5},{5,6},{6,7},{7,8},{8,9},{9,10},{10,1... | collective-permute-start | bytes 1966088 | tf_op jit(solution)/shard_map/ppermute | solution.py:13
  349.5 61.8 %collective-permute-start.4 = (bf16[128,2560]{1,0:T(8,128)(2,1)S(1)}, bf16[128,2560]{1,0:T(8,128)(2,1)S(1)}, u32[]{:S(2)}, u32[]{:S(2)}) collective-permute-start(bf16[128,2560]{1,0:T(8,128)(2,1)S(1)} %slice.8), channel_id=1, source_target_pairs={{1,0},{2,1},{3,2},{4,3},{5,4},{6,5},{7,6},{8,7},{9,8},{10,9},{11,1... | collective-permute-start | bytes 1966088 | tf_op jit(solution)/shard_map/ppermute | solution.py:13
  425.9 8.9 %slice-start = ((bf16[128,3840]{1,0:T(8,128)(2,1)}), bf16[128,1280]{1,0:T(8,128)(2,1)S(1)}, s32[]{:S(2)}) async-start(bf16[128,3840]{1,0:T(8,128)(2,1)} %copy-done), calls=%async_computation.4 | async-start | bytes 655360 | tf_op jit(solution)/shard_map/slice | solution.py:29
  478.7 45.7 %all-to-all-start.2 = ((f32[1,128,20]{2,0,1:T(1,128)}), f32[1,128,20]{2,0,1:T(1,128)S(1)}, u32[]{:S(2)}, u32[]{:S(2)}) async-start(f32[1,128,20]{2,0,1:T(1,128)} %copy.49), calls=%async_computation.2 | async-start | bytes 131072 | tf_op jit(solution)/shard_map/all_to_all | solution.py:97
  524.5 17.8 %all-to-all-start = ((f32[1,128,20]{2,0,1:T(1,128)}), f32[1,128,20]{2,0,1:T(1,128)S(1)}, u32[]{:S(2)}, u32[]{:S(2)}) async-start(f32[1,128,20]{2,0,1:T(1,128)} %copy.44), calls=%async_computation | async-start | bytes 131072 | tf_op jit(solution)/shard_map/all_to_all | solution.py:96
  542.3 44.7 %all-to-all-start.1 = ((f32[64,1,2560]{2,1,0:T(1,128)}), f32[64,1,2560]{2,1,0:T(1,128)S(1)}, u32[]{:S(2)}, u32[]{:S(2)}) async-start(f32[64,1,2560]{2,1,0:T(1,128)} %reshape.137), calls=%async_computation.1 | async-start | bytes 1310720 | tf_op jit(solution)/shard_map/all_to_all | solution.py:95
Sparse Core Ops, SparseCore 0:
  10.1 136.0 all-gather.4
where the time goes:
time: 602 us; the launch traced here: 600 us
  blocking collectives  230 us (38%)
  starting transfers between devices  131 us (22%)
  waiting for transfers between devices  123 us (20%)
  local copies, waits for them, and re-layouts  56.6 us (9%)
  matrix products  30.5 us (5%)
  between operations  14.5 us (2%)
  other arithmetic  10.7 us (2%)
    all_gather x1, blocking collectives, on_device(): all_masks = lax.all_gather(stretch_mask, 'tm', axis=0, tiled=True)  116 us
    all_gather x1, blocking collectives, on_device(): all_queries = lax.all_gather(dec_queries, 'tm', axis=0, tiled=True)  114 us
    ppermute x16, starting transfers between devices, from_behind(): return lax.ppermute(block, axis, route)  83.2 us
    ppermute x16, waiting for transfers between devices, from_behind(): return lax.ppermute(block, axis, route)  74.5 us
    unnamed x30, local copies, waits for them, and re-layouts  35.9 us
    all_to_all x1, starting transfers between devices, on_device(): lax.all_to_all(denom[None], 'tm', split_axis=1, concat_axis=0, tiled=True)  32.9 us
    all_to_all x1, waiting for transfers between devices, on_device(): lax.all_to_all(numer[None], 'tm', split_axis=1, concat_axis=0, tiled=True)  32.7 us
    all_to_all x1, waiting for transfers between devices, on_device(): lax.all_to_all(denom[None], 'tm', split_axis=1, concat_axis=0, tiled=True)  12.1 us
  transfers between devices with their start and end apart: 20, of which 9 were waited for; matrix products, arithmetic and copies ran while one was open for 7% of the time, Pallas kernels for 0%

commit v1 on v0

--- a/solution.py
+++ b/solution.py
@@ -67,7 +67,15 @@
     memory = (values_in + context).astype(jnp.bfloat16)
     tokens_dev = dec_queries.shape[0]
     all_queries = lax.all_gather(dec_queries, "tm", axis=0, tiled=True)
-    all_masks = lax.all_gather(stretch_mask, "tm", axis=0, tiled=True)
+    all_masks = jnp.concatenate(
+        lax.all_to_all(
+            jnp.stack(lax.axis_size("tm") * [stretch_mask]),
+            axis_name="tm",
+            split_axis=0,
+            concat_axis=0,
+        ),
+        axis=0,
+    )
     total_tokens = all_queries.shape[0]
     device = lax.axis_index("tm")
     column = lax.dynamic_slice_in_dim(all_masks, device, 1, 1)[:, 0]

time: 602 us -> 516 us (0.86)
  blocking collectives: 230 us -> 126 us
  starting transfers between devices: 131 us -> 147 us
    all_gather x1 -> x0, blocking collectives: 116 us -> none  [on_device(): all_masks = lax.all_gather(stretch_mask, 'tm', axis=0, tiled=True)]
    all_to_all x0 -> x1, starting transfers between devices: none -> 16.9 us  [on_device(): lax.all_to_all(jnp.stack(lax.axis_size('tm') * [stretch_mask]), axis_name...]
    all_gather x1, blocking collectives: 114 us -> 126 us  [on_device(): all_queries = lax.all_gather(dec_queries, 'tm', axis=0, tiled=True)]
    unnamed x30 -> x31, local copies, waits for them, and re-layouts: 35.9 us -> 38.7 us
  transfers between devices with their start and end apart: 20 -> 21, of which waited for: 9 -> 8; matrix products, arithmetic and copies ran while one was open for 7% -> 9% of each run, Pallas kernels for 0% -> 0%
where the time goes in v1:
time: 516 us; the launch traced here: 514 us
  starting transfers between devices  147 us (28%)
  blocking collectives  126 us (24%)
  waiting for transfers between devices  119 us (23%)
  local copies, waits for them, and re-layouts  60.6 us (12%)
  matrix products  30.5 us (6%)
  between operations  14.5 us (3%)
  other arithmetic  11.5 us (2%)
    all_gather x1, blocking collectives, on_device(): all_queries = lax.all_gather(dec_queries, 'tm', axis=0, tiled=True)  126 us
    ppermute x16, starting transfers between devices, from_behind(): return lax.ppermute(block, axis, route)  83.5 us
    ppermute x16, waiting for transfers between devices, from_behind(): return lax.ppermute(block, axis, route)  70.8 us
    unnamed x31, local copies, waits for them, and re-layouts  38.7 us
    all_to_all x1, waiting for transfers between devices, on_device(): lax.all_to_all(numer[None], 'tm', split_axis=1, concat_axis=0, tiled=True)  32.7 us
    all_to_all x1, starting transfers between devices, on_device(): lax.all_to_all(denom[None], 'tm', split_axis=1, concat_axis=0, tiled=True)  31.9 us
    all_to_all x1, starting transfers between devices, on_device(): lax.all_to_all(jnp.stack(lax.axis_size('tm') * [stretch_mask]), axis_name...  16.9 us
    all_to_all x1, waiting for transfers between devices, on_device(): lax.all_to_all(denom[None], 'tm', split_axis=1, concat_axis=0, tiled=True)  12.1 us
  transfers between devices with their start and end apart: 21, of which 8 were waited for; matrix products, arithmetic and copies ran while one was open for 9% of the time, Pallas kernels for 0%

profile of v1, /device:TPU:1, one launch (start us, length us, event | category | flops | bytes accessed | tf_op | source)
XLA Modules:
  0.0 513.6 jit_solution(3773944787560098799)
XLA Ops:
  10.5 8.7 %collective-permute-start.12 = (s32[128]{0:T(128)}, s32[128]{0:T(128)S(1)}, u32[]{:S(2)}, u32[]{:S(2)}) collective-permute-start(s32[128]{0:T(128)} %param.11), channel_id=1, source_target_pairs={{1,0},{2,1},{3,2},{4,3},{5,4},{6,5},{7,6},{8,7},{9,8},{10,9},{11,1... | collective-permute-start | bytes 1544 | tf_op jit(solution)/shard_map/ppermute | solution.py:13
  19.3 4.2 collective-permute-start.11
  23.4 5.2 %collective-permute-start.8 = (s32[128]{0:T(128)}, s32[128]{0:T(128)S(1)}, u32[]{:S(2)}, u32[]{:S(2)}) collective-permute-start(s32[128]{0:T(128)} %param.11), channel_id=1, source_target_pairs={{0,4},{1,5},{2,6},{3,7},{4,8},{5,9},{6,10},{7,11},{8,12},{9,13},{1... | collective-permute-start | bytes 1544 | tf_op jit(solution)/shard_map/ppermute | solution.py:13
  30.0 16.9 %all-to-all-start = ((s32[64,1,128]{2,1,0:T(1,128)}), s32[64,1,128]{2,1,0:T(1,128)S(1)}, u32[]{:S(2)}, u32[]{:S(2)}) async-start(s32[64,1,128]{2,1,0:T(1,128)} %reshape.142), calls=%async_computation | async-start | bytes 65536 | tf_op jit(solution)/shard_map/all_to_all | solution.py:71
  48.5 126.3 %all-gather.1 = bf16[64,2,1280]{2,1,0:T(2,128)(2,1)S(1)} all-gather(bf16[1,2,1280]{2,1,0:T(2,128)(2,1)} %bitcast.70), channel_id=1, replica_groups=mesh['utt'=8,'tm'=64] {'tm'}, dimensions={0}, use_global_device_ids=true | all-gather | bytes 332800 | tf_op jit(solution)/shard_map/all_gather | solution.py:69
  177.5 3.9 collective-permute-start.10
  183.5 13.7 %reshape.134 = bf16[1280,3840]{1,0:T(8,128)(2,1)} reshape(bf16[64,20,3840]{2,1,0:T(8,128)(2,1)} %all-gather.4.cloned.1.call-done) | data formatting | bytes 19660800
  197.2 5.3 %convolution_convert_fusion = bf16[128,3840]{1,0:T(8,128)(2,1)S(1)} fusion(bf16[1280,3840]{1,0:T(8,128)(2,1)} %reshape.134, bf16[128,1280]{0,1:T(8,128)(2,1)S(1)} %copy.46, f32[1280]{0:T(1024)S(1)} %copy-done.2, f32[128]{0:T(128)S(1)} %add_rsqrt_fusion, f32[128]{0:T(128)S(1)} %broadcast_multiply_fusion), kind=kOutput, calls=%fused_computation.16 | convolution fusion | flops 1259601920 | bytes 11147264 | tf_op jit(solution)/shard_map/dot_general | solution.py:24
  202.6 5.7 %collective-permute-start = (bf16[128,2560]{1,0:T(8,128)(2,1)S(1)}, bf16[128,2560]{1,0:T(8,128)(2,1)}, u32[]{:S(2)}, u32[]{:S(2)}) collective-permute-start(bf16[128,2560]{1,0:T(8,128)(2,1)S(1)} %slice.8), channel_id=1, source_target_pairs={{0,4},{1,5},{2,6},{3,7},{4,8},{5,9},{6,10},{7,11},{8,12},{9,13},{1... | collective-permute-start | bytes 1966088 | tf_op jit(solution)/shard_map/ppermute | solution.py:13
  208.4 7.7 %collective-permute-start.1 = (bf16[128,2560]{1,0:T(8,128)(2,1)S(1)}, bf16[128,2560]{1,0:T(8,128)(2,1)}, u32[]{:S(2)}, u32[]{:S(2)}) collective-permute-start(bf16[128,2560]{1,0:T(8,128)(2,1)S(1)} %slice.8), channel_id=1, source_target_pairs={{0,3},{1,4},{2,5},{3,6},{4,7},{5,8},{6,9},{7,10},{8,11},{9,12},{10... | collective-permute-start | bytes 1966088 | tf_op jit(solution)/shard_map/ppermute | solution.py:13
  221.5 24.6 %collective-permute-start.2 = (bf16[128,2560]{1,0:T(8,128)(2,1)S(1)}, bf16[128,2560]{1,0:T(8,128)(2,1)S(1)}, u32[]{:S(2)}, u32[]{:S(2)}) collective-permute-start(bf16[128,2560]{1,0:T(8,128)(2,1)S(1)} %slice.8), channel_id=1, source_target_pairs={{0,2},{1,3},{2,4},{3,5},{4,6},{5,7},{6,8},{7,9},{8,10},{9,11},{10,... | collective-permute-start | bytes 1966088 | tf_op jit(solution)/shard_map/ppermute | solution.py:13
  248.1 12.5 %collective-permute-start.3 = (bf16[128,2560]{1,0:T(8,128)(2,1)S(1)}, bf16[128,2560]{1,0:T(8,128)(2,1)S(1)}, u32[]{:S(2)}, u32[]{:S(2)}) collective-permute-start(bf16[128,2560]{1,0:T(8,128)(2,1)S(1)} %slice.8), channel_id=1, source_target_pairs={{0,1},{1,2},{2,3},{3,4},{4,5},{5,6},{6,7},{7,8},{8,9},{9,10},{10,1... | collective-permute-start | bytes 1966088 | tf_op jit(solution)/shard_map/ppermute | solution.py:13
  265.4 2.7 collective-permute-done.3
  270.0 54.6 %collective-permute-done.4 = bf16[128,2560]{1,0:T(8,128)(2,1)S(1)} collective-permute-done((bf16[128,2560]{1,0:T(8,128)(2,1)S(1)}, bf16[128,2560]{1,0:T(8,128)(2,1)S(1)}, u32[]{:S(2)}, u32[]{:S(2)}) %collective-permute-start.4) | collective-permute-done | bytes 655392 | tf_op jit(solution)/shard_map/ppermute | solution.py:13
  326.3 12.1 %collective-permute-done.6 = bf16[128,2560]{1,0:T(8,128)(2,1)S(1)} collective-permute-done((bf16[128,2560]{1,0:T(8,128)(2,1)S(1)}, bf16[128,2560]{1,0:T(8,128)(2,1)S(1)}, u32[]{:S(2)}, u32[]{:S(2)}) %collective-permute-start.6) | collective-permute-done | bytes 655392 | tf_op jit(solution)/shard_map/ppermute | solution.py:13
  340.2 8.9 %copy.47 = bf16[1152,2560]{0,1:T(8,128)(2,1)} copy(bf16[1152,2560]{1,0:T(8,128)(2,1)} %constant_dynamic-update-slice_fusion.1) | data formatting | bytes 11796480
  349.1 41.2 %while.13 = (s32[]{:T(128)}, f32[5,128,256]{1,2,0:T(8,128)}, s32[5]{0:T(128)S(1)}, bf16[1152,2560]{0,1:T(8,128)(2,1)}, bf16[128,1280]{1,0:T(8,128)(2,1)S(1)}, /*...) while((s32[]{:T(128)}, f32[5,128,256]{1,2,0:T(8,128)}, ...), condition=%wide.region_5.6_spmd.clone, body=%wide.region_2.5_spmd.clone.sunk | while | flops 154682496 | bytes 9282826 | solution.py:65
  393.1 31.9 %all-to-all-start.3 = ((f32[1,128,20]{2,0,1:T(1,128)}), f32[1,128,20]{2,0,1:T(1,128)S(1)}, u32[]{:S(2)}, u32[]{:S(2)}) async-start(f32[1,128,20]{2,0,1:T(1,128)} %copy.55), calls=%async_computation.3 | async-start | bytes 131072 | tf_op jit(solution)/shard_map/all_to_all | solution.py:105
  425.7 12.1 %all-to-all-done.3 = f32[1,128,20]{2,0,1:T(1,128)S(1)} async-done(((f32[1,128,20]{2,0,1:T(1,128)}), f32[1,128,20]{2,0,1:T(1,128)S(1)}, u32[]{:S(2)}, u32[]{:S(2)}) %all-to-all-start.3) | async-done | bytes 10272 | tf_op jit(solution)/shard_map/all_to_all | solution.py:105
  437.8 5.0 all-to-all-start.1
  447.0 3.9 reduce.3
  452.6 3.0 all-to-all-done.1
  455.6 10.0 %all-to-all-start.2 = ((f32[64,1,2560]{2,1,0:T(1,128)}), f32[64,1,2560]{2,1,0:T(1,128)S(1)}, u32[]{:S(2)}, u32[]{:S(2)}) async-start(f32[64,1,2560]{2,1,0:T(1,128)} %reshape.144), calls=%async_computation.2 | async-start | bytes 1310720 | tf_op jit(solution)/shard_map/all_to_all | solution.py:103
  467.6 32.7 %all-to-all-done.2 = f32[64,1,2560]{2,1,0:T(1,128)S(1)} async-done(((f32[64,1,2560]{2,1,0:T(1,128)}), f32[64,1,2560]{2,1,0:T(1,128)S(1)}, u32[]{:S(2)}, u32[]{:S(2)}) %all-to-all-start.2) | async-done | bytes 655392 | tf_op jit(solution)/shard_map/all_to_all | solution.py:103
  (130 shorter events, 83.9 us)
Async XLA Ops:
  7.2 168.3 %copy-start.1 = (s32[128]{0:T(128)S(1)}, s32[128]{0:T(128)}, u32[]{:S(2)}) copy-start(s32[128]{0:T(128)} %param.11) | copy-start | bytes 1540
  7.2 176.3 %all-gather.4.cloned.1.call-start = ((), (), s32[]{:S(2)}) async-start(), calls=%async_computation.4 | async-start | bytes 11980800 | tf_op jit(solution)/shard_map/all_gather | solution.py:26
  7.9 200.4 %collective-permute-start.14 = (s32[128]{0:T(128)}, s32[128]{0:T(128)S(1)}, u32[]{:S(2)}, u32[]{:S(2)}) collective-permute-start(s32[128]{0:T(128)} %param.11), channel_id=1, source_target_pairs={{3,0},{4,1},{5,2},{6,3},{7,4},{8,5},{9,6},{10,7},{11,8},{12,9},{13... | collective-permute-start | bytes 1544 | tf_op jit(solution)/shard_map/ppermute | solution.py:13
  9.2 199.1 %collective-permute-start.13 = (s32[128]{0:T(128)}, s32[128]{0:T(128)S(1)}, u32[]{:S(2)}, u32[]{:S(2)}) collective-permute-start(s32[128]{0:T(128)} %param.11), channel_id=1, source_target_pairs={{2,0},{3,1},{4,2},{5,3},{6,4},{7,5},{8,6},{9,7},{10,8},{11,9},{12,... | collective-permute-start | bytes 1544 | tf_op jit(solution)/shard_map/ppermute | solution.py:13
  10.5 197.8 %collective-permute-start.12 = (s32[128]{0:T(128)}, s32[128]{0:T(128)S(1)}, u32[]{:S(2)}, u32[]{:S(2)}) collective-permute-start(s32[128]{0:T(128)} %param.11), channel_id=1, source_target_pairs={{1,0},{2,1},{3,2},{4,3},{5,4},{6,5},{7,6},{8,7},{9,8},{10,9},{11,1... | collective-permute-start | bytes 1544 | tf_op jit(solution)/shard_map/ppermute | solution.py:13
  19.3 164.1 %collective-permute-start.11 = (s32[128]{0:T(128)}, s32[128]{0:T(128)S(1)}, u32[]{:S(2)}, u32[]{:S(2)}) collective-permute-start(s32[128]{0:T(128)} %param.11), channel_id=1, source_target_pairs={{0,1},{1,2},{2,3},{3,4},{4,5},{5,6},{6,7},{7,8},{8,9},{9,10},{10,1... | collective-permute-start | bytes 1544 | tf_op jit(solution)/shard_map/ppermute | solution.py:13
  23.4 152.0 %collective-permute-start.8 = (s32[128]{0:T(128)}, s32[128]{0:T(128)S(1)}, u32[]{:S(2)}, u32[]{:S(2)}) collective-permute-start(s32[128]{0:T(128)} %param.11), channel_id=1, source_target_pairs={{0,4},{1,5},{2,6},{3,7},{4,8},{5,9},{6,10},{7,11},{8,12},{9,13},{1... | collective-permute-start | bytes 1544 | tf_op jit(solution)/shard_map/ppermute | solution.py:13
  30.0 186.0 %all-to-all-start = ((s32[64,1,128]{2,1,0:T(1,128)}), s32[64,1,128]{2,1,0:T(1,128)S(1)}, u32[]{:S(2)}, u32[]{:S(2)}) async-start(s32[64,1,128]{2,1,0:T(1,128)} %reshape.142), calls=%async_computation | async-start | bytes 65536 | tf_op jit(solution)/shard_map/all_to_all | solution.py:71
  175.5 2.0 collective-permute-start.9
  177.5 4.6 collective-permute-start.10
  182.1 33.9 %collective-permute-start.15 = (s32[128]{0:T(128)S(1)}, s32[128]{0:T(128)S(1)}, u32[]{:S(2)}, u32[]{:S(2)}) collective-permute-start(s32[128]{0:T(128)S(1)} %copy-done.1), channel_id=1, source_target_pairs={{4,0},{5,1},{6,2},{7,3},{8,4},{9,5},{10,6},{11,7},{12,8},{13,9},{1... | collective-permute-start | bytes 1544 | tf_op jit(solution)/shard_map/ppermute | solution.py:13
  183.4 13.7 %copy-start.2 = (f32[1280]{0:T(1024)S(1)}, f32[1280]{0:T(1024)}, u32[]{:S(2)}) copy-start(f32[1280]{0:T(1024)} %param.9) | copy-start | bytes 15364
  202.5 66.5 %copy-start = (bf16[128,3840]{1,0:T(8,128)(2,1)}, bf16[128,3840]{1,0:T(8,128)(2,1)S(1)}, u32[]{:S(2)}) copy-start(bf16[128,3840]{1,0:T(8,128)(2,1)S(1)} %convolution_convert_fusion) | copy-start | bytes 2949124
  202.6 18.9 %collective-permute-start = (bf16[128,2560]{1,0:T(8,128)(2,1)S(1)}, bf16[128,2560]{1,0:T(8,128)(2,1)}, u32[]{:S(2)}, u32[]{:S(2)}) collective-permute-start(bf16[128,2560]{1,0:T(8,128)(2,1)S(1)} %slice.8), channel_id=1, source_target_pairs={{0,4},{1,5},{2,6},{3,7},{4,8},{5,9},{6,10},{7,11},{8,12},{9,13},{1... | collective-permute-start | bytes 1966088 | tf_op jit(solution)/shard_map/ppermute | solution.py:13
  208.4 39.7 %collective-permute-start.1 = (bf16[128,2560]{1,0:T(8,128)(2,1)S(1)}, bf16[128,2560]{1,0:T(8,128)(2,1)}, u32[]{:S(2)}, u32[]{:S(2)}) collective-permute-start(bf16[128,2560]{1,0:T(8,128)(2,1)S(1)} %slice.8), channel_id=1, source_target_pairs={{0,3},{1,4},{2,5},{3,6},{4,7},{5,8},{6,9},{7,10},{8,11},{9,12},{10... | collective-permute-start | bytes 1966088 | tf_op jit(solution)/shard_map/ppermute | solution.py:13
  217.6 121.8 %collective-permute-start.7 = (bf16[128,2560]{1,0:T(8,128)(2,1)S(1)}, bf16[128,2560]{1,0:T(8,128)(2,1)S(1)}, u32[]{:S(2)}, u32[]{:S(2)}) collective-permute-start(bf16[128,2560]{1,0:T(8,128)(2,1)S(1)} %slice.8), channel_id=1, source_target_pairs={{4,0},{5,1},{6,2},{7,3},{8,4},{9,5},{10,6},{11,7},{12,8},{13,9},{1... | collective-permute-start | bytes 1966088 | tf_op jit(solution)/shard_map/ppermute | solution.py:13
  218.9 119.6 %collective-permute-start.6 = (bf16[128,2560]{1,0:T(8,128)(2,1)S(1)}, bf16[128,2560]{1,0:T(8,128)(2,1)S(1)}, u32[]{:S(2)}, u32[]{:S(2)}) collective-permute-start(bf16[128,2560]{1,0:T(8,128)(2,1)S(1)} %slice.8), channel_id=1, source_target_pairs={{3,0},{4,1},{5,2},{6,3},{7,4},{8,5},{9,6},{10,7},{11,8},{12,9},{13... | collective-permute-start | bytes 1966088 | tf_op jit(solution)/shard_map/ppermute | solution.py:13
  220.2 105.2 %collective-permute-start.5 = (bf16[128,2560]{1,0:T(8,128)(2,1)S(1)}, bf16[128,2560]{1,0:T(8,128)(2,1)S(1)}, u32[]{:S(2)}, u32[]{:S(2)}) collective-permute-start(bf16[128,2560]{1,0:T(8,128)(2,1)S(1)} %slice.8), channel_id=1, source_target_pairs={{2,0},{3,1},{4,2},{5,3},{6,4},{7,5},{8,6},{9,7},{10,8},{11,9},{12,... | collective-permute-start | bytes 1966088 | tf_op jit(solution)/shard_map/ppermute | solution.py:13
  221.5 41.1 %collective-permute-start.2 = (bf16[128,2560]{1,0:T(8,128)(2,1)S(1)}, bf16[128,2560]{1,0:T(8,128)(2,1)S(1)}, u32[]{:S(2)}, u32[]{:S(2)}) collective-permute-start(bf16[128,2560]{1,0:T(8,128)(2,1)S(1)} %slice.8), channel_id=1, source_target_pairs={{0,2},{1,3},{2,4},{3,5},{4,6},{5,7},{6,8},{7,9},{8,10},{9,11},{10,... | collective-permute-start | bytes 1966088 | tf_op jit(solution)/shard_map/ppermute | solution.py:13
  248.1 20.0 %collective-permute-start.3 = (bf16[128,2560]{1,0:T(8,128)(2,1)S(1)}, bf16[128,2560]{1,0:T(8,128)(2,1)S(1)}, u32[]{:S(2)}, u32[]{:S(2)}) collective-permute-start(bf16[128,2560]{1,0:T(8,128)(2,1)S(1)} %slice.8), channel_id=1, source_target_pairs={{0,1},{1,2},{2,3},{3,4},{4,5},{5,6},{6,7},{7,8},{8,9},{9,10},{10,1... | collective-permute-start | bytes 1966088 | tf_op jit(solution)/shard_map/ppermute | solution.py:13
  262.6 61.9 %collective-permute-start.4 = (bf16[128,2560]{1,0:T(8,128)(2,1)S(1)}, bf16[128,2560]{1,0:T(8,128)(2,1)S(1)}, u32[]{:S(2)}, u32[]{:S(2)}) collective-permute-start(bf16[128,2560]{1,0:T(8,128)(2,1)S(1)} %slice.8), channel_id=1, source_target_pairs={{1,0},{2,1},{3,2},{4,3},{5,4},{6,5},{7,6},{8,7},{9,8},{10,9},{11,1... | collective-permute-start | bytes 1966088 | tf_op jit(solution)/shard_map/ppermute | solution.py:13
  393.1 44.7 %all-to-all-start.3 = ((f32[1,128,20]{2,0,1:T(1,128)}), f32[1,128,20]{2,0,1:T(1,128)S(1)}, u32[]{:S(2)}, u32[]{:S(2)}) async-start(f32[1,128,20]{2,0,1:T(1,128)} %copy.55), calls=%async_computation.3 | async-start | bytes 131072 | tf_op jit(solution)/shard_map/all_to_all | solution.py:105
  437.8 17.8 %all-to-all-start.1 = ((f32[1,128,20]{2,0,1:T(1,128)}), f32[1,128,20]{2,0,1:T(1,128)S(1)}, u32[]{:S(2)}, u32[]{:S(2)}) async-start(f32[1,128,20]{2,0,1:T(1,128)} %copy.50), calls=%async_computation.1 | async-start | bytes 131072 | tf_op jit(solution)/shard_map/all_to_all | solution.py:104
  455.6 44.7 %all-to-all-start.2 = ((f32[64,1,2560]{2,1,0:T(1,128)}), f32[64,1,2560]{2,1,0:T(1,128)S(1)}, u32[]{:S(2)}, u32[]{:S(2)}) async-start(f32[64,1,2560]{2,1,0:T(1,128)} %reshape.144), calls=%async_computation.2 | async-start | bytes 1310720 | tf_op jit(solution)/shard_map/all_to_all | solution.py:103
  (1 other events, 8.9 us)
Sparse Core Ops, SparseCore 0:
  10.1 137.9 all-gather.3
